TPU v7x, 32 devices: a whole 2x2x4 slice. The times are simulated.
32 devices in a mesh: tm: 8 (over z, y), tensor: 4 (over x, core).
Axes of the slice: x: 2, y: 2, z: 4, core: 2. Of those that a mesh axis runs over, the one named last changes fastest.
Arguments:
- frames_in: bfloat16 [8, 528, 1024], P('tm'), may hold values from -6 to 6
- frame_time: int32 [8], replicated, may hold values from 0 to 7, each once
- cond_count: int32 [8], replicated, may hold values from 0 to 2
- ln1_gain: float32 [2, 1024], replicated, may hold values from 0.5 to 1.5
- ln1_bias: float32 [2, 1024], replicated, may hold values from -1.75 to 1.75
- qkv_weight: bfloat16 [2, 3, 1024, 1024], P(None, None, None, 'tensor'), may hold values from -17 to 17
- qkv_bias: float32 [2, 3, 1024], P(None, None, 'tensor'), may hold values from -1.75 to 1.75
- out_weight: bfloat16 [2, 1024, 1024], P(None, 'tensor'), may hold values from -0.1875 to 0.1875
- out_bias: float32 [2, 1024], replicated, may hold values from -1.75 to 1.75
- ln2_gain: float32 [2, 1024], replicated, may hold values from 0.5 to 1.5
- ln2_bias: float32 [2, 1024], replicated, may hold values from -1.75 to 1.75
- fc1_weight: bfloat16 [2, 1024, 4096], P(None, None, 'tensor'), may hold values from -0.1875 to 0.1875
- fc1_bias: float32 [2, 4096], P(None, 'tensor'), may hold values from -3 to 3
- fc2_weight: bfloat16 [2, 4096, 1024], P(None, 'tensor'), may hold values from -0.09375 to 0.09375
- fc2_bias: float32 [2, 1024], replicated, may hold values from -1.75 to 1.75
Outputs:
- frames_out: bfloat16 [8, 528, 1024], P('tm', 'tensor')
Inputs may be any that keep to these rules, and one draw needn't show every extreme that they name: `frame_time`: every time index 0 to 7 appears once. `cond_count`: the valid action and state tokens of a frame are its first ones.
All inputs are finite; a program needn't handle non-finite values.
Results may differ from a plain program's by a relative error of at most 0.04.
Values may be sent and summed in bfloat16 or wider, within the bound.
A program may use at most 128 MiB of HBM per device.

v0:
```python
import jax
import jax.numpy as jnp
from jax import lax
from jax.sharding import PartitionSpec as P

D = 1024
HEADS = 16
PATCH_DEV = 64
COND = 2
LAYERS = 2


def layer_norm(inputs, gain_row, bias_row):
    center = jnp.mean(inputs, axis=-1, keepdims=True)
    spread = jnp.mean(jnp.square(inputs - center), axis=-1, keepdims=True)
    return (inputs - center) * lax.rsqrt(spread + 1e-06) * gain_row + bias_row


def piece_tables(frame_time, cond_count, piece_count, frame_split, piece_rows):
    cond_dev = COND // frame_split
    piece_ids = jnp.arange(piece_count, dtype=jnp.int32)
    frame_ids = jnp.arange(frame_time.shape[0], dtype=jnp.int32)
    matches = (piece_ids // frame_split)[:, None] == frame_ids[None, :]
    piece_time = jnp.sum(jnp.where(matches, frame_time[None, :], 0), axis=1)
    piece_cond = jnp.sum(jnp.where(matches, cond_count[None, :], 0), axis=1)
    slot_index = jnp.arange(piece_rows, dtype=jnp.int32)
    cond_slot = (piece_ids % frame_split)[:, None] * cond_dev + slot_index[None, :] - PATCH_DEV
    valid = (slot_index[None, :] < PATCH_DEV) | (cond_slot < piece_cond[:, None])
    return (piece_time, valid)


def shards_gather(
    frames_in,
    frame_time,
    cond_count,
    ln1_gain,
    ln1_bias,
    qkv_weight,
    qkv_bias,
    out_weight,
    out_bias,
    ln2_gain,
    ln2_bias,
    fc1_weight,
    fc1_bias,
    fc2_weight,
    fc2_bias,
):
    frame_count = frame_time.shape[0]
    piece_count = lax.axis_size("tm")
    frame_split = piece_count // frame_count
    cond_dev = COND // frame_split
    piece_rows = PATCH_DEV + cond_dev
    row_count = frames_in.shape[1]
    seq_count = row_count // piece_rows
    head_dim = D // HEADS
    head_local = qkv_weight.shape[3] // head_dim
    scale = head_dim ** (-0.5)
    tensor_size = lax.axis_size("tensor")
    tensor_pos = lax.axis_index("tensor")
    my_piece = lax.axis_index("tm")
    share_rows = row_count // tensor_size
    piece_time, valid = piece_tables(frame_time, cond_count, piece_count, frame_split, piece_rows)
    piece_ids = jnp.arange(piece_count, dtype=jnp.int32)
    my_time = jnp.sum(jnp.where(piece_ids == my_piece, piece_time, 0))
    full_in = frames_in[0]
    new_share = None
    for layer_idx in range(LAYERS):
        normed = layer_norm(
            full_in.astype(jnp.float32), ln1_gain[layer_idx], ln1_bias[layer_idx]
        ).astype(jnp.bfloat16)
        projected = jnp.einsum(
            "rd,jde->jre", normed, qkv_weight[layer_idx], preferred_element_type=jnp.float32
        )
        projected = (projected + qkv_bias[layer_idx][:, None, :]).astype(jnp.bfloat16)
        queries = projected[0].reshape(seq_count, piece_rows, head_local, head_dim)
        keys_mine = projected[1].reshape(1, seq_count, piece_rows, head_local * head_dim)
        values_mine = projected[2].reshape(1, seq_count, piece_rows, head_local * head_dim)
        start_top = jnp.full((seq_count, head_local, piece_rows), -1e30, jnp.float32)
        key_block = lax.all_gather(keys_mine, "tm", axis=0, tiled=True)
        value_block = lax.all_gather(values_mine, "tm", axis=0, tiled=True)
        block_count = key_block.shape[0]
        block_ids = jnp.arange(block_count, dtype=jnp.int32)
        matches = block_ids[:, None] == piece_ids[None, :]
        key_time = jnp.sum(jnp.where(matches, piece_time[None, :], 0), axis=1)
        key_valid = jnp.any(matches[:, :, None] & valid[None, :, :], axis=1)
        allowed = (key_time <= my_time)[:, None] & key_valid
        top_run = start_top
        keys_split = key_block.reshape(block_count, seq_count, piece_rows, head_local, head_dim)
        values_split = value_block.reshape(block_count, seq_count, piece_rows, head_local, head_dim)
        scores = (
            jnp.einsum("sqhd,gskhd->shqgk", queries, keys_split, preferred_element_type=jnp.float32)
            * scale
        )
        scores = jnp.where(allowed, scores, -1e30)
        new_top = jnp.maximum(top_run, jnp.max(scores, axis=(3, 4)))
        weights = jnp.where(allowed, jnp.exp(scores - new_top[..., None, None]), 0.0)
        total_new = jnp.sum(weights, axis=(3, 4))
        mixed = jnp.einsum(
            "shqgk,gskhd->shqd",
            weights.astype(jnp.bfloat16),
            values_split,
            preferred_element_type=jnp.float32,
        )
        top_run = new_top
        attended = (
            (mixed / total_new[..., None])
            .transpose(0, 2, 1, 3)
            .reshape(row_count, head_local * head_dim)
            .astype(jnp.bfloat16)
        )
        out_layer = out_weight[layer_idx]
        fc1_layer = fc1_weight[layer_idx]
        fc2_layer = fc2_weight[layer_idx]
        fc1_layer_bias = fc1_bias[layer_idx]
        own_rows = lax.dynamic_slice_in_dim(full_in, tensor_pos * share_rows, share_rows, 0).astype(
            jnp.float32
        )
        first = (
            own_rows
            + lax.psum_scatter(
                jnp.dot(attended, out_layer, preferred_element_type=jnp.float32).astype(
                    jnp.bfloat16
                ),
                "tensor",
                scatter_dimension=0,
                tiled=True,
            ).astype(jnp.float32)
            + out_bias[layer_idx]
        )
        normed_two = layer_norm(first, ln2_gain[layer_idx], ln2_bias[layer_idx]).astype(
            jnp.bfloat16
        )
        inner = jax.nn.gelu(
            jnp.dot(
                lax.all_gather(normed_two, "tensor", axis=0, tiled=True),
                fc1_layer,
                preferred_element_type=jnp.float32,
            )
            + fc1_layer_bias,
            approximate=False,
        ).astype(jnp.bfloat16)
        mlp_share = lax.psum_scatter(
            jnp.dot(inner, fc2_layer, preferred_element_type=jnp.float32).astype(jnp.bfloat16),
            "tensor",
            scatter_dimension=0,
            tiled=True,
        ).astype(jnp.float32)
        new_share = (first + mlp_share + fc2_bias[layer_idx]).astype(jnp.bfloat16)
        if layer_idx + 1 < LAYERS:
            full_in = lax.all_gather(new_share, "tensor", axis=0, tiled=True)
    return new_share[None]


def shards_clip(
    frames_in,
    frame_time,
    cond_count,
    ln1_gain,
    ln1_bias,
    qkv_weight,
    qkv_bias,
    out_weight,
    out_bias,
    ln2_gain,
    ln2_bias,
    fc1_weight,
    fc1_bias,
    fc2_weight,
    fc2_bias,
):
    frame_count = frame_time.shape[0]
    piece_count = lax.axis_size("tm")
    frame_split = piece_count // frame_count
    piece_rows = PATCH_DEV + COND // frame_split
    row_count = frames_in.shape[1]
    seq_count = row_count // piece_rows
    clips = seq_count // piece_count
    head_dim = D // HEADS
    head_local = qkv_weight.shape[3] // head_dim
    scale = head_dim ** (-0.5)
    tensor_size = lax.axis_size("tensor")
    tensor_pos = lax.axis_index("tensor")
    share_rows = row_count // tensor_size
    share_cols = D // tensor_size
    piece_time, valid = piece_tables(frame_time, cond_count, piece_count, frame_split, piece_rows)
    row_time = jnp.repeat(piece_time, piece_rows)
    allowed = (row_time[None, :] <= row_time[:, None]) & valid.reshape(1, -1)
    clip_rows = piece_count * piece_rows
    mine = lax.dynamic_slice_in_dim(frames_in[0], tensor_pos * share_cols, share_cols, 1)
    mine = mine.reshape(piece_count, clips, piece_rows, share_cols)
    mine = lax.all_to_all(mine, "tm", 0, 0, tiled=True)
    mine = mine.transpose(1, 0, 2, 3).reshape(row_count, share_cols)
    full_in = lax.all_gather(mine, "tensor", axis=1, tiled=True)
    new_share = None
    for layer_idx in range(LAYERS):
        normed = layer_norm(
            full_in.astype(jnp.float32), ln1_gain[layer_idx], ln1_bias[layer_idx]
        ).astype(jnp.bfloat16)
        parts = []
        for i in range(3):
            part = jnp.dot(normed, qkv_weight[layer_idx, i], preferred_element_type=jnp.float32)
            part = (part + qkv_bias[layer_idx, i]).astype(jnp.bfloat16)
            parts.append(part.reshape(clips, clip_rows, head_local, head_dim))
        queries, keys, values = parts
        scores = (
            jnp.einsum("sqhd,skhd->shqk", queries, keys, preferred_element_type=jnp.float32) * scale
        )
        scores = jnp.where(allowed, scores, -1e30)
        top = jnp.max(scores, axis=-1, keepdims=True)
        weights = jnp.where(allowed, jnp.exp(scores - top), 0.0)
        total = jnp.sum(weights, axis=-1, keepdims=True)
        mixed = jnp.einsum(
            "shqk,skhd->shqd",
            weights.astype(jnp.bfloat16),
            values,
            preferred_element_type=jnp.float32,
        )
        attended = (
            (mixed / total)
            .transpose(0, 2, 1, 3)
            .reshape(row_count, head_local * head_dim)
            .astype(jnp.bfloat16)
        )
        own_rows = lax.dynamic_slice_in_dim(full_in, tensor_pos * share_rows, share_rows, 0).astype(
            jnp.float32
        )
        first = (
            own_rows
            + lax.psum_scatter(
                jnp.dot(attended, out_weight[layer_idx], preferred_element_type=jnp.float32).astype(
                    jnp.bfloat16
                ),
                "tensor",
                scatter_dimension=0,
                tiled=True,
            ).astype(jnp.float32)
            + out_bias[layer_idx]
        )
        normed_two = layer_norm(first, ln2_gain[layer_idx], ln2_bias[layer_idx]).astype(
            jnp.bfloat16
        )
        inner = jax.nn.gelu(
            jnp.dot(
                lax.all_gather(normed_two, "tensor", axis=0, tiled=True),
                fc1_weight[layer_idx],
                preferred_element_type=jnp.float32,
            )
            + fc1_bias[layer_idx],
            approximate=False,
        ).astype(jnp.bfloat16)
        mlp_share = lax.psum_scatter(
            jnp.dot(inner, fc2_weight[layer_idx], preferred_element_type=jnp.float32).astype(
                jnp.bfloat16
            ),
            "tensor",
            scatter_dimension=0,
            tiled=True,
        ).astype(jnp.float32)
        new_share = (first + mlp_share + fc2_bias[layer_idx]).astype(jnp.bfloat16)
        if layer_idx + 1 < LAYERS:
            full_in = lax.all_gather(new_share, "tensor", axis=0, tiled=True)
    cols = jnp.stack(jnp.split(new_share, tensor_size, axis=1))
    cols = lax.all_to_all(cols, "tensor", 0, 0, tiled=True)
    cols = cols.reshape(clips, piece_count, piece_rows, share_cols).transpose(1, 0, 2, 3)
    cols = lax.all_to_all(cols, "tm", 0, 0, tiled=True)
    cols = cols.reshape(tensor_size, share_rows, share_cols)
    cols = lax.all_to_all(cols, "tensor", 0, 0, tiled=True)
    out = cols.transpose(1, 0, 2).reshape(share_rows, D)
    return out[None]


def shards(frames_in, frame_time, cond_count, *rest):
    frame_split = lax.axis_size("tm") // frame_time.shape[0]
    piece_rows = PATCH_DEV + COND // frame_split
    seq_count = frames_in.shape[1] // piece_rows
    by_clip = seq_count % lax.axis_size("tm") == 0
    body = shards_clip if by_clip else shards_gather
    return body(frames_in, frame_time, cond_count, *rest)


def solution(mesh):
    in_specs = (
        P("tm", None, None),
        P(),
        P(),
        P(),
        P(),
        P(None, None, None, "tensor"),
        P(None, None, "tensor"),
        P(None, "tensor", None),
        P(),
        P(),
        P(),
        P(None, None, "tensor"),
        P(None, "tensor"),
        P(None, "tensor", None),
        P(),
    )
    out_specs = P("tm", "tensor", None)
    return jax.shard_map(shards, mesh=mesh, in_specs=in_specs, out_specs=out_specs, check_vma=False)
```

profile of v0, /device:TPU:0, one launch (start us, length us, event | category | flops | bytes accessed | tf_op | source)
XLA Modules:
  0.0 282.2 jit_solution(10008635543005344850)
XLA Ops:
  8.6 7.3 %all-to-all-start = ((bf16[8,1,66,256]{3,2,1,0:T(8,128)(2,1)}), bf16[8,1,66,256]{3,2,1,0:T(8,128)(2,1)S(1)}, u32[]{:S(2)}, u32[]{:S(2)}) async-start(bf16[8,1,66,256]{3,2,1,0:T(8,128)(2,1)} %bitcast), calls=%async_computation | async-start | bytes 589824 | tf_op jit(solution)/shard_map/all_to_all | solution.py:192
  17.5 8.0 %all-to-all-done = bf16[8,1,66,256]{3,2,1,0:T(8,128)(2,1)S(1)} async-done(((bf16[8,1,66,256]{3,2,1,0:T(8,128)(2,1)}), bf16[8,1,66,256]{3,2,1,0:T(8,128)(2,1)S(1)}, u32[]{:S(2)}, u32[]{:S(2)}) %all-to-all-start) | async-done | bytes 270368 | tf_op jit(solution)/shard_map/all_to_all | solution.py:192
  30.8 11.8 %all-gather.8.cloned.1.call-done = bf16[528,1024]{1,0:T(8,128)(2,1)} async-done(((bf16[528,256]{1,0:T(8,128)(2,1)}), bf16[528,1024]{1,0:T(8,128)(2,1)}) %all-gather.8.cloned.1.call-update) | async-done | bytes 1081360 | tf_op jit(solution)/shard_map/all_gather | solution.py:194
  42.5 1.6 convert_reduce_fusion.1
  44.1 1.7 fusion.26
  46.2 1.5 fusion.82
  48.7 1.5 fusion.80
  51.0 1.5 fusion.81
  52.8 5.4 %fusion.256 = (f32[4,528]{1,0:T(4,128)S(1)}, bf16[4,528,528]{1,2,0:T(8,128)(2,1)}) fusion(pred[528,528]{0,1:T(8,128)(4,1)} %compare_and_fusion, bf16[528,4,64]{0,2,1:T(8,128)(2,1)} %bitcast.137, bf16[528,4,64]{0,2,1:T(8,128)(2,1)S(1)} %bitcast.139), kind=kOutput, calls=%fused_computation.290 | convolution fusion | flops 149428752 | bytes 3058176 | tf_op jit(solution)/shard_map/sub | solution.py:211
  58.2 2.5 fusion.77
  61.2 15.4 %fusion = bf16[136,1024]{1,0:T(8,128)(2,1)S(1)} fusion(bf16[528,1024]{1,0:T(8,128)(2,1)S(1)} %convolution_convert_fusion.1), kind=kCustom, calls=%all-reduce-scatter | all-reduce-scatter fusion | flops 557057 | bytes 1360384
  82.6 18.1 %all-gather.10.cloned.1.call-done = bf16[4,132,1024]{2,1,0:T(8,128)(2,1)} async-done(((bf16[1,132,1024]{2,1,0:T(8,128)(2,1)}), bf16[4,132,1024]{2,1,0:T(8,128)(2,1)}) %all-gather.10.cloned.1.call-update) | async-done | bytes 1081360 | tf_op jit(solution)/shard_map/all_gather | solution.py:245
  100.7 1.3 reshape.189
  102.1 9.7 %fusion.62 = bf16[528,1024]{1,0:T(8,128)(2,1)} fusion(bf16[2,1024,1024]{2,1,0:T(8,128)(2,1)} %param.28, f32[1024]{0:T(1024)} %bitcast.161, bf16[528,1024]{1,0:T(8,128)(2,1)S(1)} %reshape.189, bf16[2,1024,1024]{2,1,0:T(8,128)(2,1)} %param.26), kind=kOutput, calls=%fused_computation.84 | convolution fusion | flops 2250817536 | bytes 6361088 | tf_op jit(solution)/shard_map/dot_general | solution.py:253
  111.8 15.9 %fusion.1 = bf16[136,1024]{1,0:T(8,128)(2,1)S(1)} fusion(bf16[528,1024]{1,0:T(8,128)(2,1)} %fusion.62), kind=kCustom, calls=%all-reduce-scatter.1 | all-reduce-scatter fusion | flops 557057 | bytes 1360384
  129.0 1.4 fusion.248
  130.7 1.6 fusion.181
  132.7 19.2 %all-gather.12.cloned.1.call-done = bf16[4,132,1024]{2,1,0:T(8,128)(2,1)} async-done(((bf16[1,132,1024]{2,1,0:T(8,128)(2,1)}), bf16[4,132,1024]{2,1,0:T(8,128)(2,1)}) %all-gather.12.cloned.1.call-update) | async-done | bytes 1081360 | tf_op jit(solution)/shard_map/all_gather | solution.py:262
  151.9 1.3 reshape.191
  154.5 1.5 fusion.85
  156.9 1.5 fusion.83
  159.3 1.5 fusion.84
  161.0 5.4 %fusion.257 = (f32[4,528]{1,0:T(4,128)S(1)}, bf16[4,528,528]{1,2,0:T(8,128)(2,1)}) fusion(pred[528,528]{0,1:T(8,128)(4,1)} %compare_and_fusion, bf16[528,4,64]{0,2,1:T(8,128)(2,1)} %bitcast.136, bf16[528,4,64]{0,2,1:T(8,128)(2,1)S(1)} %bitcast.138), kind=kOutput, calls=%fused_computation.291 | convolution fusion | flops 149428752 | bytes 3058176 | tf_op jit(solution)/shard_map/sub | solution.py:211
  166.4 2.5 fusion.74
  169.4 15.4 %fusion.2 = bf16[136,1024]{1,0:T(8,128)(2,1)S(1)} fusion(bf16[528,1024]{1,0:T(8,128)(2,1)S(1)} %convolution_convert_fusion), kind=kCustom, calls=%all-reduce-scatter.2 | all-reduce-scatter fusion | flops 557057 | bytes 1360384
  184.8 1.6 collective-permute-start.2
  189.0 20.0 %all-gather.14.cloned.1.call-done = bf16[4,132,1024]{2,1,0:T(8,128)(2,1)} async-done(((bf16[1,132,1024]{2,1,0:T(8,128)(2,1)}), bf16[4,132,1024]{2,1,0:T(8,128)(2,1)}) %all-gather.14.cloned.1.call-update) | async-done | bytes 1081360 | tf_op jit(solution)/shard_map/all_gather | solution.py:245
  210.3 9.7 %fusion.65 = bf16[528,1024]{1,0:T(8,128)(2,1)} fusion(bf16[2,1024,1024]{2,1,0:T(8,128)(2,1)} %param.28, f32[1024]{0:T(1024)} %bitcast.160, bf16[528,1024]{1,0:T(8,128)(2,1)S(1)} %reshape.193, bf16[2,1024,1024]{2,1,0:T(8,128)(2,1)} %param.26), kind=kOutput, calls=%fused_computation.85 | convolution fusion | flops 2250817536 | bytes 6361088 | tf_op jit(solution)/shard_map/dot_general | solution.py:253
  220.1 15.9 %fusion.3 = bf16[136,1024]{1,0:T(8,128)(2,1)S(1)} fusion(bf16[528,1024]{1,0:T(8,128)(2,1)} %fusion.65), kind=kCustom, calls=%all-reduce-scatter.3 | all-reduce-scatter fusion | flops 557057 | bytes 1360384
  239.5 10.7 %all_to_all.20 = bf16[4,132,256]{2,1,0:T(8,128)(2,1)S(1)} all-to-all(bf16[4,132,256]{2,1,0:T(8,128)(2,1)S(1)} %pad_maximum_fusion), channel_id=1, replica_groups=mesh['tm'=8,'tensor'=4] {'tensor'}, dimensions={0} | all-to-all | bytes 540672 | tf_op jit(solution)/shard_map/all_to_all | solution.py:264
  250.2 15.8 %all_to_all.21 = bf16[8,1,66,256]{3,2,1,0:T(8,128)(2,1)S(1)} all-to-all(bf16[8,1,66,256]{3,2,1,0:T(8,128)(2,1)S(1)} %bitcast.132), channel_id=1, replica_groups=mesh['tm'=8,'tensor'=4] {'tm'}, dimensions={0} | all-to-all | bytes 540672 | tf_op jit(solution)/shard_map/all_to_all | solution.py:266
  266.1 8.5 %all_to_all.22 = bf16[4,132,256]{2,1,0:T(8,128)(2,1)S(1)} all-to-all(bf16[4,132,256]{2,1,0:T(8,128)(2,1)S(1)} %reshape.187), channel_id=1, replica_groups=mesh['tm'=8,'tensor'=4] {'tensor'}, dimensions={0} | all-to-all | bytes 540672 | tf_op jit(solution)/shard_map/all_to_all | solution.py:268
  (122 shorter events, 31.2 us)
Async XLA Ops:
  6.5 1.2 copy-start
  6.5 20.2 %copy-start.18 = (f32[2,3,256]{2,0,1:T(2,128)S(1)}, f32[2,3,256]{2,0,1:T(2,128)}, u32[]{:S(2)}) copy-start(f32[2,3,256]{2,0,1:T(2,128)} %param.21) | copy-start | bytes 18436
  6.5 20.8 %copy-start.12 = (f32[2,1024]{1,0:T(2,128)S(1)}, f32[2,1024]{1,0:T(2,128)}, u32[]{:S(2)}) copy-start(f32[2,1024]{1,0:T(2,128)} %param.25) | copy-start | bytes 24580
  6.5 21.4 %copy-start.13 = (f32[2,1024]{1,0:T(2,128)S(1)}, f32[2,1024]{1,0:T(2,128)}, u32[]{:S(2)}) copy-start(f32[2,1024]{1,0:T(2,128)} %param.24) | copy-start | bytes 24580
  6.5 22.0 %copy-start.14 = (f32[2,1024]{1,0:T(2,128)S(1)}, f32[2,1024]{1,0:T(2,128)}, u32[]{:S(2)}) copy-start(f32[2,1024]{1,0:T(2,128)} %param.19) | copy-start | bytes 24580
  6.5 22.6 %copy-start.15 = (f32[2,1024]{1,0:T(2,128)S(1)}, f32[2,1024]{1,0:T(2,128)}, u32[]{:S(2)}) copy-start(f32[2,1024]{1,0:T(2,128)} %param.18) | copy-start | bytes 24580
  8.6 16.9 %all-to-all-start = ((bf16[8,1,66,256]{3,2,1,0:T(8,128)(2,1)}), bf16[8,1,66,256]{3,2,1,0:T(8,128)(2,1)S(1)}, u32[]{:S(2)}, u32[]{:S(2)}) async-start(bf16[8,1,66,256]{3,2,1,0:T(8,128)(2,1)} %bitcast), calls=%async_computation | async-start | bytes 589824 | tf_op jit(solution)/shard_map/all_to_all | solution.py:192
  15.9 26.6 %all-gather.8.cloned.1.call-start = ((), (), s32[]{:S(2)}) async-start(), calls=%async_computation.4 | async-start | bytes 1351680 | tf_op jit(solution)/shard_map/all_gather | solution.py:194
  26.3 74.4 %all-gather.10.cloned.1.call-start = ((), (), s32[]{:S(2)}) async-start(), calls=%async_computation.5 | async-start | bytes 1392640 | tf_op jit(solution)/shard_map/all_gather | solution.py:245
  42.5 3.3 %copy-start.1 = (bf16[528,1024]{1,0:T(8,128)(2,1)S(1)}, bf16[528,1024]{1,0:T(8,128)(2,1)}, u32[]{:S(2)}) copy-start(bf16[528,1024]{1,0:T(8,128)(2,1)} %all-gather.8.cloned.1.call-done) | copy-start | bytes 3244036
  52.7 5.4 %copy-start.5 = (bf16[528,256]{0,1:T(8,128)(2,1)S(1)}, bf16[528,256]{0,1:T(8,128)(2,1)}, u32[]{:S(2)}) copy-start(bf16[528,256]{0,1:T(8,128)(2,1)} %copy.56) | copy-start | bytes 811012
  58.2 2.5 copy-start.2
  60.7 17.2 %copy-start.16 = (f32[2,1024]{1,0:T(2,128)S(1)}, f32[2,1024]{1,0:T(2,128)}, u32[]{:S(2)}) copy-start(f32[2,1024]{1,0:T(2,128)} %param.23) | copy-start | bytes 24580
  60.7 17.8 %copy-start.22 = (u32[32]{0:T(128)S(1)}, u32[32]{0:T(128)}, u32[]{:S(2)}) copy-start(u32[32]{0:T(128)} %constant.128) | copy-start | bytes 388
  61.2 20.8 %copy-start.17 = (f32[2,1024]{1,0:T(2,128)S(1)}, f32[2,1024]{1,0:T(2,128)}, u32[]{:S(2)}) copy-start(f32[2,1024]{1,0:T(2,128)} %param.27) | copy-start | bytes 24580
  76.6 3.1 %collective-permute-start = (bf16[12,1024]{1,0:T(8,128)(2,1)S(1)}, bf16[12,1024]{1,0:T(8,128)(2,1)S(1)}, u32[]{:S(2)}, u32[]{:S(2)}) collective-permute-start(bf16[12,1024]{1,0:T(8,128)(2,1)S(1)} %slice.128), channel_id=1, source_target_pairs={{0,1},{1,2},{2,3},{4,5},{5,6},{6,7},{8,9},{9,10},{10,11},{12,13},{... | collective-permute-start | bytes 73736
  78.5 4.1 %copy-start.7 = (f32[1,1024]{1,0:T(1,128)}, f32[1,1024]{1,0:T(1,128)S(1)}, u32[]{:S(2)}) copy-start(f32[1,1024]{1,0:T(1,128)S(1)} %get-tuple-element.15) | copy-start | bytes 12292
  81.8 70.1 %all-gather.12.cloned.1.call-start = ((), (), s32[]{:S(2)}) async-start(), calls=%async_computation.6 | async-start | bytes 1392640 | tf_op jit(solution)/shard_map/all_gather | solution.py:262
  127.7 2.7 collective-permute-start.1
  132.4 21.6 %copy-start.10 = (f32[1,1024]{1,0:T(1,128)S(1)}, f32[1,1024]{1,0:T(1,128)}, u32[]{:S(2)}) copy-start(f32[1,1024]{1,0:T(1,128)} %get-tuple-element.13) | copy-start | bytes 12292
  132.4 21.6 %copy-start.11 = (f32[1,1024]{1,0:T(1,128)S(1)}, f32[1,1024]{1,0:T(1,128)}, u32[]{:S(2)}) copy-start(f32[1,1024]{1,0:T(1,128)} %get-tuple-element.11) | copy-start | bytes 12292
  132.4 76.6 %all-gather.14.cloned.1.call-start = ((), (), s32[]{:S(2)}) async-start(), calls=%async_computation.7 | async-start | bytes 1392640 | tf_op jit(solution)/shard_map/all_gather | solution.py:245
  153.3 1.2 copy-start.21
  154.0 2.9 %copy-start.20 = (f32[1,1,256]{2,0,1:T(1,128)S(1)}, f32[1,1,256]{2,0,1:T(1,128)}, u32[]{:S(2)}) copy-start(f32[1,1,256]{2,0,1:T(1,128)} %get-tuple-element.24) | copy-start | bytes 3076
  156.0 3.3 %copy-start.19 = (f32[1,1,256]{2,0,1:T(1,128)S(1)}, f32[1,1,256]{2,0,1:T(1,128)}, u32[]{:S(2)}) copy-start(f32[1,1,256]{2,0,1:T(1,128)} %get-tuple-element.23) | copy-start | bytes 3076
  161.0 5.4 %copy-start.4 = (bf16[528,256]{0,1:T(8,128)(2,1)S(1)}, bf16[528,256]{0,1:T(8,128)(2,1)}, u32[]{:S(2)}) copy-start(bf16[528,256]{0,1:T(8,128)(2,1)} %copy.60) | copy-start | bytes 811012
  166.4 2.5 copy-start.3
  168.9 18.4 %copy-start.6 = (f32[1,1024]{1,0:T(1,128)S(1)}, f32[1,1024]{1,0:T(1,128)}, u32[]{:S(2)}) copy-start(f32[1,1024]{1,0:T(1,128)} %get-tuple-element.16) | copy-start | bytes 12292
  169.0 18.9 %copy-start.8 = (f32[1,1024]{1,0:T(1,128)S(1)}, f32[1,1024]{1,0:T(1,128)}, u32[]{:S(2)}) copy-start(f32[1,1024]{1,0:T(1,128)} %get-tuple-element.20) | copy-start | bytes 12292
  169.0 18.9 %copy-start.9 = (f32[1,1024]{1,0:T(1,128)S(1)}, f32[1,1024]{1,0:T(1,128)}, u32[]{:S(2)}) copy-start(f32[1,1024]{1,0:T(1,128)} %get-tuple-element.18) | copy-start | bytes 12292
  184.8 2.1 collective-permute-start.2
  236.0 2.1 collective-permute-start.3
Sparse Core Ops, SparseCore 0:
  26.4 16.0 all-gather.7
  81.9 18.7 all-gather.9
  132.5 19.3 all-gather.11
  189.1 19.8 all-gather.13
where the time goes:
time: 283 us; the launch traced here: 282 us
  blocking collectives  97.6 us (34%)
  waiting for transfers between devices  78.6 us (28%)
  matrix products  45.1 us (16%)
  local copies, waits for them, and re-layouts  19.8 us (7%)
  between operations  14.3 us (5%)
  other arithmetic  13.4 us (5%)
  starting transfers between devices  13.3 us (5%)
    unnamed x4, blocking collectives  62.5 us
    all_gather x2, waiting for transfers between devices, shards_clip(): lax.all_gather(normed_two, 'tensor', axis=0, tiled=True)  38.1 us
    dot_general x2, matrix products, shards_clip(): jnp.dot(inner, fc2_weight[layer_idx], preferred_element_type=jnp.float32)  19.5 us
    all_gather x1, waiting for transfers between devices, shards_clip(): full_in = lax.all_gather(new_share, 'tensor', axis=0, tiled=True)  19.2 us
    all_to_all x2, blocking collectives, shards_clip(): cols = lax.all_to_all(cols, 'tensor', 0, 0, tiled=True)  19.2 us
    all_to_all x1, blocking collectives, shards_clip(): cols = lax.all_to_all(cols, 'tm', 0, 0, tiled=True)  15.8 us
    all_gather x1, waiting for transfers between devices, shards_clip(): full_in = lax.all_gather(mine, 'tensor', axis=1, tiled=True)  11.8 us
    sub x2, matrix products, shards_clip(): weights = jnp.where(allowed, jnp.exp(scores - top), 0.0)  10.8 us
  transfers between devices with their start and end apart: 9, of which 7 were waited for; matrix products, arithmetic and copies ran while one was open for 3% of the time, Pallas kernels for 0%

commit v1 on v0

--- a/solution.py
+++ b/solution.py
@@ -8,6 +8,27 @@
 PATCH_DEV = 64
 COND = 2
 LAYERS = 2
+
+
+def laid_out(blocks, dim):
+    shape = list(blocks.shape[1:])
+    shape[dim] *= blocks.shape[0]
+    return jnp.moveaxis(blocks, 0, dim).reshape(shape)
+
+
+def collected_by_bits(x, axis):
+    size, here = (lax.axis_size(axis), lax.axis_index(axis))
+    blocks, stride = (x[None], 1)
+    while stride < size:
+        other = lax.ppermute(blocks, axis, [(i, i ^ stride) for i in range(size)])
+        low = here & stride == 0
+        blocks = jnp.concatenate([jnp.where(low, blocks, other), jnp.where(low, other, blocks)])
+        stride *= 2
+    return blocks
+
+
+def gather_by_bits(array, axis, dim):
+    return laid_out(collected_by_bits(array, axis), dim)
 
 
 def layer_norm(inputs, gain_row, bias_row):
@@ -242,7 +263,7 @@
         )
         inner = jax.nn.gelu(
             jnp.dot(
-                lax.all_gather(normed_two, "tensor", axis=0, tiled=True),
+                gather_by_bits(normed_two, "tensor", 0),
                 fc1_weight[layer_idx],
                 preferred_element_type=jnp.float32,
             )

time: 283 us -> 285 us (level)
  waiting for transfers between devices: 78.6 us -> 68.6 us
  starting transfers between devices: 13.3 us -> 19.6 us
  other arithmetic: 13.4 us -> 16.9 us
    all_gather x2 -> x0, waiting for transfers between devices: 38.1 us -> none  [shards_clip(): lax.all_gather(normed_two, 'tensor', axis=0, tiled=True)]
    ppermute x0 -> x4, waiting for transfers between devices: none -> 27.8 us  [collected_by_bits(): other = lax.ppermute(blocks, axis, [(i, i ^ stride) for i in range(size)])]
    ppermute x0 -> x4, starting transfers between devices: none -> 6.4 us  [collected_by_bits(): other = lax.ppermute(blocks, axis, [(i, i ^ stride) for i in range(size)])]
    unnamed x58 -> x56, local copies, waits for them, and re-layouts: 7.26 us -> 4.57 us
  transfers between devices with their start and end apart: 9 -> 11, of which waited for: 7 -> 9; matrix products, arithmetic and copies ran while one was open for 3% -> 3% of each run, Pallas kernels for 0% -> 0%
where the time goes in v1:
time: 285 us; the launch traced here: 284 us
  blocking collectives  97.5 us (34%)
  waiting for transfers between devices  68.6 us (24%)
  matrix products  45.1 us (16%)
  local copies, waits for them, and re-layouts  21.7 us (8%)
  starting transfers between devices  19.6 us (7%)
  other arithmetic  16.9 us (6%)
  between operations  14.6 us (5%)
    unnamed x4, blocking collectives  62.3 us
    ppermute x4, waiting for transfers between devices, collected_by_bits(): other = lax.ppermute(blocks, axis, [(i, i ^ stride) for i in range(size)])  27.8 us
    all_gather x1, waiting for transfers between devices, shards_clip(): full_in = lax.all_gather(new_share, 'tensor', axis=0, tiled=True)  19.5 us
    dot_general x2, matrix products, shards_clip(): jnp.dot(inner, fc2_weight[layer_idx], preferred_element_type=jnp.float32)  19.4 us
    all_to_all x2, blocking collectives, shards_clip(): cols = lax.all_to_all(cols, 'tensor', 0, 0, tiled=True)  19.4 us
    all_to_all x1, blocking collectives, shards_clip(): cols = lax.all_to_all(cols, 'tm', 0, 0, tiled=True)  15.8 us
    all_gather x1, waiting for transfers between devices, shards_clip(): full_in = lax.all_gather(mine, 'tensor', axis=1, tiled=True)  11.8 us
    sub x2, matrix products, shards_clip(): weights = jnp.where(allowed, jnp.exp(scores - top), 0.0)  10.9 us
  transfers between devices with their start and end apart: 11, of which 9 were waited for; matrix products, arithmetic and copies ran while one was open for 3% of the time, Pallas kernels for 0%

profile of v1, /device:TPU:0, one launch (start us, length us, event | category | flops | bytes accessed | tf_op | source)
XLA Modules:
  0.0 284.2 jit_solution(14161163533253484040)
XLA Ops:
  8.6 7.3 %all-to-all-start = ((bf16[8,1,66,256]{3,2,1,0:T(8,128)(2,1)}), bf16[8,1,66,256]{3,2,1,0:T(8,128)(2,1)S(1)}, u32[]{:S(2)}, u32[]{:S(2)}) async-start(bf16[8,1,66,256]{3,2,1,0:T(8,128)(2,1)} %bitcast), calls=%async_computation | async-start | bytes 589824 | tf_op jit(solution)/shard_map/all_to_all | solution.py:213
  17.5 8.0 %all-to-all-done = bf16[8,1,66,256]{3,2,1,0:T(8,128)(2,1)S(1)} async-done(((bf16[8,1,66,256]{3,2,1,0:T(8,128)(2,1)}), bf16[8,1,66,256]{3,2,1,0:T(8,128)(2,1)S(1)}, u32[]{:S(2)}, u32[]{:S(2)}) %all-to-all-start) | async-done | bytes 270368 | tf_op jit(solution)/shard_map/all_to_all | solution.py:213
  30.7 11.8 %all-gather.4.cloned.1.call-done = bf16[528,1024]{1,0:T(8,128)(2,1)} async-done(((bf16[528,256]{1,0:T(8,128)(2,1)}), bf16[528,1024]{1,0:T(8,128)(2,1)}) %all-gather.4.cloned.1.call-update) | async-done | bytes 1081360 | tf_op jit(solution)/shard_map/all_gather | solution.py:215
  42.5 1.6 convert_reduce_fusion.1
  44.1 1.7 fusion.26
  46.2 1.5 fusion.82
  48.7 1.5 fusion.80
  51.1 1.5 fusion.81
  52.8 5.4 %fusion.256 = (f32[4,528]{1,0:T(4,128)S(1)}, bf16[4,528,528]{1,2,0:T(8,128)(2,1)}) fusion(pred[528,528]{0,1:T(8,128)(4,1)} %compare_and_fusion, bf16[528,4,64]{0,2,1:T(8,128)(2,1)} %bitcast.137, bf16[528,4,64]{0,2,1:T(8,128)(2,1)S(1)} %bitcast.139), kind=kOutput, calls=%fused_computation.302 | convolution fusion | flops 149428752 | bytes 3058176 | tf_op jit(solution)/shard_map/sub | solution.py:232
  58.2 2.5 fusion.77
  61.2 15.4 %fusion = bf16[136,1024]{1,0:T(8,128)(2,1)S(1)} fusion(bf16[528,1024]{1,0:T(8,128)(2,1)S(1)} %convolution_convert_fusion.1), kind=kCustom, calls=%all-reduce-scatter | all-reduce-scatter fusion | flops 557057 | bytes 1360384
  86.0 1.5 collective-permute-start.1
  88.1 12.8 %collective-permute-done.1 = bf16[2,132,1024]{2,0,1:T(2,128)(2,1)} collective-permute-done((bf16[2,132,1024]{2,0,1:T(2,128)(2,1)}, bf16[2,132,1024]{2,0,1:T(2,128)(2,1)}, u32[]{:S(2)}, u32[]{:S(2)}) %collective-permute-start.1) | collective-permute-done | bytes 540704 | tf_op jit(solution)/shard_map/ppermute | solution.py:23
  104.6 9.7 %fusion.62 = bf16[528,1024]{1,0:T(8,128)(2,1)} fusion(bf16[2,1024,1024]{2,1,0:T(8,128)(2,1)} %param.28, f32[1024]{0:T(1024)} %bitcast.161, bf16[528,1024]{1,0:T(8,128)(2,1)S(1)} %reshape.190, bf16[2,1024,1024]{2,1,0:T(8,128)(2,1)} %param.26), kind=kOutput, calls=%fused_computation.84 | convolution fusion | flops 2250817536 | bytes 6361088 | tf_op jit(solution)/shard_map/dot_general | solution.py:274
  114.4 15.5 %fusion.1 = bf16[136,1024]{1,0:T(8,128)(2,1)S(1)} fusion(bf16[528,1024]{1,0:T(8,128)(2,1)} %fusion.62), kind=kCustom, calls=%all-reduce-scatter.1 | all-reduce-scatter fusion | flops 557057 | bytes 1360384
  129.9 1.5 collective-permute-start.5
  133.2 1.7 fusion.181
  134.9 19.5 %all-gather.6.cloned.1.call-done = bf16[4,132,1024]{2,1,0:T(8,128)(2,1)} async-done(((bf16[1,132,1024]{2,1,0:T(8,128)(2,1)}), bf16[4,132,1024]{2,1,0:T(8,128)(2,1)}) %all-gather.6.cloned.1.call-update) | async-done | bytes 1081360 | tf_op jit(solution)/shard_map/all_gather | solution.py:283
  156.9 1.5 fusion.85
  159.4 1.5 fusion.83
  161.8 1.5 fusion.84
  163.5 5.4 %fusion.257 = (f32[4,528]{1,0:T(4,128)S(1)}, bf16[4,528,528]{1,2,0:T(8,128)(2,1)}) fusion(pred[528,528]{0,1:T(8,128)(4,1)} %compare_and_fusion, bf16[528,4,64]{0,2,1:T(8,128)(2,1)} %bitcast.136, bf16[528,4,64]{0,2,1:T(8,128)(2,1)S(1)} %bitcast.138), kind=kOutput, calls=%fused_computation.303 | convolution fusion | flops 149428752 | bytes 3058176 | tf_op jit(solution)/shard_map/sub | solution.py:232
  168.9 2.5 fusion.74
  171.9 15.4 %fusion.2 = bf16[136,1024]{1,0:T(8,128)(2,1)S(1)} fusion(bf16[528,1024]{1,0:T(8,128)(2,1)S(1)} %convolution_convert_fusion), kind=kCustom, calls=%all-reduce-scatter.2 | all-reduce-scatter fusion | flops 557057 | bytes 1360384
  187.3 1.6 collective-permute-start.6
  193.8 2.6 collective-permute-start.3
  196.5 12.6 %collective-permute-done.3 = bf16[2,132,1024]{2,0,1:T(2,128)(2,1)S(1)} collective-permute-done((bf16[2,132,1024]{2,0,1:T(2,128)(2,1)S(1)}, bf16[2,132,1024]{2,0,1:T(2,128)(2,1)S(1)}, u32[]{:S(2)}, u32[]{:S(2)}) %collective-permute-start.3) | collective-permute-done | bytes 540704 | tf_op jit(solution)/shard_map/ppermute | solution.py:23
  211.7 9.7 %fusion.65 = bf16[528,1024]{1,0:T(8,128)(2,1)} fusion(bf16[2,1024,1024]{2,1,0:T(8,128)(2,1)} %param.28, f32[1024]{0:T(1024)} %bitcast.160, bf16[528,1024]{1,0:T(8,128)(2,1)S(1)} %reshape.194, bf16[2,1024,1024]{2,1,0:T(8,128)(2,1)} %param.26), kind=kOutput, calls=%fused_computation.85 | convolution fusion | flops 2250817536 | bytes 6361088 | tf_op jit(solution)/shard_map/dot_general | solution.py:274
  221.4 16.0 %fusion.3 = bf16[136,1024]{1,0:T(8,128)(2,1)S(1)} fusion(bf16[528,1024]{1,0:T(8,128)(2,1)} %fusion.65), kind=kCustom, calls=%all-reduce-scatter.3 | all-reduce-scatter fusion | flops 557057 | bytes 1360384
  240.9 10.9 %all_to_all.20 = bf16[4,132,256]{2,1,0:T(8,128)(2,1)S(1)} all-to-all(bf16[4,132,256]{2,1,0:T(8,128)(2,1)S(1)} %pad_maximum_fusion.4), channel_id=1, replica_groups=mesh['tm'=8,'tensor'=4] {'tensor'}, dimensions={0} | all-to-all | bytes 540672 | tf_op jit(solution)/shard_map/all_to_all | solution.py:285
  251.9 15.8 %all_to_all.21 = bf16[8,1,66,256]{3,2,1,0:T(8,128)(2,1)S(1)} all-to-all(bf16[8,1,66,256]{3,2,1,0:T(8,128)(2,1)S(1)} %bitcast.132), channel_id=1, replica_groups=mesh['tm'=8,'tensor'=4] {'tm'}, dimensions={0} | all-to-all | bytes 540672 | tf_op jit(solution)/shard_map/all_to_all | solution.py:287
  267.8 8.5 %all_to_all.22 = bf16[4,132,256]{2,1,0:T(8,128)(2,1)S(1)} all-to-all(bf16[4,132,256]{2,1,0:T(8,128)(2,1)S(1)} %reshape.195), channel_id=1, replica_groups=mesh['tm'=8,'tensor'=4] {'tensor'}, dimensions={0} | all-to-all | bytes 540672 | tf_op jit(solution)/shard_map/all_to_all | solution.py:289
  (134 shorter events, 43.7 us)
Async XLA Ops:
  6.5 20.2 %copy-start.18 = (f32[2,3,256]{2,0,1:T(2,128)S(1)}, f32[2,3,256]{2,0,1:T(2,128)}, u32[]{:S(2)}) copy-start(f32[2,3,256]{2,0,1:T(2,128)} %param.21) | copy-start | bytes 18436
  6.5 20.8 %copy-start.12 = (f32[2,1024]{1,0:T(2,128)S(1)}, f32[2,1024]{1,0:T(2,128)}, u32[]{:S(2)}) copy-start(f32[2,1024]{1,0:T(2,128)} %param.25) | copy-start | bytes 24580
  6.5 21.4 %copy-start.13 = (f32[2,1024]{1,0:T(2,128)S(1)}, f32[2,1024]{1,0:T(2,128)}, u32[]{:S(2)}) copy-start(f32[2,1024]{1,0:T(2,128)} %param.24) | copy-start | bytes 24580
  6.5 22.0 %copy-start.14 = (f32[2,1024]{1,0:T(2,128)S(1)}, f32[2,1024]{1,0:T(2,128)}, u32[]{:S(2)}) copy-start(f32[2,1024]{1,0:T(2,128)} %param.19) | copy-start | bytes 24580
  6.5 22.6 %copy-start.15 = (f32[2,1024]{1,0:T(2,128)S(1)}, f32[2,1024]{1,0:T(2,128)}, u32[]{:S(2)}) copy-start(f32[2,1024]{1,0:T(2,128)} %param.18) | copy-start | bytes 24580
  8.6 16.9 %all-to-all-start = ((bf16[8,1,66,256]{3,2,1,0:T(8,128)(2,1)}), bf16[8,1,66,256]{3,2,1,0:T(8,128)(2,1)S(1)}, u32[]{:S(2)}, u32[]{:S(2)}) async-start(bf16[8,1,66,256]{3,2,1,0:T(8,128)(2,1)} %bitcast), calls=%async_computation | async-start | bytes 589824 | tf_op jit(solution)/shard_map/all_to_all | solution.py:213
  15.9 26.6 %all-gather.4.cloned.1.call-start = ((), (), s32[]{:S(2)}) async-start(), calls=%async_computation.4 | async-start | bytes 1351680 | tf_op jit(solution)/shard_map/all_gather | solution.py:215
  26.3 128.0 %all-gather.6.cloned.1.call-start = ((), (), s32[]{:S(2)}) async-start(), calls=%async_computation.5 | async-start | bytes 1392640 | tf_op jit(solution)/shard_map/all_gather | solution.py:283
  42.5 3.3 %copy-start.1 = (bf16[528,1024]{1,0:T(8,128)(2,1)S(1)}, bf16[528,1024]{1,0:T(8,128)(2,1)}, u32[]{:S(2)}) copy-start(bf16[528,1024]{1,0:T(8,128)(2,1)} %all-gather.4.cloned.1.call-done) | copy-start | bytes 3244036
  52.7 5.4 %copy-start.5 = (bf16[528,256]{0,1:T(8,128)(2,1)S(1)}, bf16[528,256]{0,1:T(8,128)(2,1)}, u32[]{:S(2)}) copy-start(bf16[528,256]{0,1:T(8,128)(2,1)} %copy.62) | copy-start | bytes 811012
  58.2 2.5 copy-start.2
  60.7 17.4 %copy-start.16 = (f32[2,1024]{1,0:T(2,128)S(1)}, f32[2,1024]{1,0:T(2,128)}, u32[]{:S(2)}) copy-start(f32[2,1024]{1,0:T(2,128)} %param.23) | copy-start | bytes 24580
  60.7 18.0 %copy-start.22 = (u32[32]{0:T(128)S(1)}, u32[32]{0:T(128)}, u32[]{:S(2)}) copy-start(u32[32]{0:T(128)} %constant.131) | copy-start | bytes 388
  76.6 3.3 %collective-permute-start.4 = (bf16[12,1024]{1,0:T(8,128)(2,1)S(1)}, bf16[12,1024]{1,0:T(8,128)(2,1)S(1)}, u32[]{:S(2)}, u32[]{:S(2)}) collective-permute-start(bf16[12,1024]{1,0:T(8,128)(2,1)S(1)} %slice.128), channel_id=1, source_target_pairs={{0,1},{1,2},{2,3},{4,5},{5,6},{6,7},{8,9},{9,10},{10,11},{12,13},{... | collective-permute-start | bytes 73736
  78.7 3.7 %copy-start.7 = (f32[1,1024]{1,0:T(1,128)}, f32[1,1024]{1,0:T(1,128)S(1)}, u32[]{:S(2)}) copy-start(f32[1,1024]{1,0:T(1,128)S(1)} %get-tuple-element.23) | copy-start | bytes 12292
  80.9 6.7 %copy-start.17 = (f32[2,1024]{1,0:T(2,128)S(1)}, f32[2,1024]{1,0:T(2,128)}, u32[]{:S(2)}) copy-start(f32[2,1024]{1,0:T(2,128)} %param.27) | copy-start | bytes 24580
  81.3 2.4 collective-permute-start
  86.0 14.9 %collective-permute-start.1 = (bf16[2,132,1024]{2,0,1:T(2,128)(2,1)}, bf16[2,132,1024]{2,0,1:T(2,128)(2,1)}, u32[]{:S(2)}, u32[]{:S(2)}) collective-permute-start(bf16[2,132,1024]{2,0,1:T(2,128)(2,1)} %copy.64), channel_id=1, source_target_pairs={{0,2},{1,3},{2,0},{3,1},{4,6},{5,7},{6,4},{7,5},{8,10},{9,11},{10,... | collective-permute-start | bytes 1622024 | tf_op jit(solution)/shard_map/ppermute | solution.py:23
  129.9 2.9 %collective-permute-start.5 = (bf16[12,1024]{1,0:T(8,128)(2,1)S(1)}, bf16[12,1024]{1,0:T(8,128)(2,1)S(1)}, u32[]{:S(2)}, u32[]{:S(2)}) collective-permute-start(bf16[12,1024]{1,0:T(8,128)(2,1)S(1)} %slice.129), channel_id=1, source_target_pairs={{0,1},{1,2},{2,3},{4,5},{5,6},{6,7},{8,9},{9,10},{10,11},{12,13},{... | collective-permute-start | bytes 73736
  134.8 21.6 %copy-start.10 = (f32[1,1024]{1,0:T(1,128)S(1)}, f32[1,1024]{1,0:T(1,128)}, u32[]{:S(2)}) copy-start(f32[1,1024]{1,0:T(1,128)} %get-tuple-element.21) | copy-start | bytes 12292
  134.8 21.6 %copy-start.11 = (f32[1,1024]{1,0:T(1,128)S(1)}, f32[1,1024]{1,0:T(1,128)}, u32[]{:S(2)}) copy-start(f32[1,1024]{1,0:T(1,128)} %get-tuple-element.19) | copy-start | bytes 12292
  156.4 2.9 %copy-start.20 = (f32[1,1,256]{2,0,1:T(1,128)S(1)}, f32[1,1,256]{2,0,1:T(1,128)}, u32[]{:S(2)}) copy-start(f32[1,1,256]{2,0,1:T(1,128)} %get-tuple-element.32) | copy-start | bytes 3076
  158.4 3.3 %copy-start.19 = (f32[1,1,256]{2,0,1:T(1,128)S(1)}, f32[1,1,256]{2,0,1:T(1,128)}, u32[]{:S(2)}) copy-start(f32[1,1,256]{2,0,1:T(1,128)} %get-tuple-element.31) | copy-start | bytes 3076
  163.5 5.4 %copy-start.4 = (bf16[528,256]{0,1:T(8,128)(2,1)S(1)}, bf16[528,256]{0,1:T(8,128)(2,1)}, u32[]{:S(2)}) copy-start(bf16[528,256]{0,1:T(8,128)(2,1)} %copy.69) | copy-start | bytes 811012
  168.9 2.5 copy-start.3
  171.4 18.4 %copy-start.6 = (f32[1,1024]{1,0:T(1,128)S(1)}, f32[1,1024]{1,0:T(1,128)}, u32[]{:S(2)}) copy-start(f32[1,1024]{1,0:T(1,128)} %get-tuple-element.24) | copy-start | bytes 12292
  171.4 18.9 %copy-start.8 = (f32[1,1024]{1,0:T(1,128)S(1)}, f32[1,1024]{1,0:T(1,128)}, u32[]{:S(2)}) copy-start(f32[1,1024]{1,0:T(1,128)} %get-tuple-element.28) | copy-start | bytes 12292
  171.4 18.9 %copy-start.9 = (f32[1,1024]{1,0:T(1,128)S(1)}, f32[1,1024]{1,0:T(1,128)}, u32[]{:S(2)}) copy-start(f32[1,1024]{1,0:T(1,128)} %get-tuple-element.26) | copy-start | bytes 12292
  187.3 2.1 collective-permute-start.6
  190.8 2.4 collective-permute-start.2
  193.8 15.2 %collective-permute-start.3 = (bf16[2,132,1024]{2,0,1:T(2,128)(2,1)S(1)}, bf16[2,132,1024]{2,0,1:T(2,128)(2,1)S(1)}, u32[]{:S(2)}, u32[]{:S(2)}) collective-permute-start(bf16[2,132,1024]{2,0,1:T(2,128)(2,1)S(1)} %copy.71), channel_id=1, source_target_pairs={{0,2},{1,3},{2,0},{3,1},{4,6},{5,7},{6,4},{7,5},{8,10},{9,11},{10,... | collective-permute-start | bytes 1622024 | tf_op jit(solution)/shard_map/ppermute | solution.py:23
  237.5 2.1 collective-permute-start.7
  (2 other events, 2.4 us)
Sparse Core Ops, SparseCore 0:
  26.4 16.0 all-gather.3
  135.0 19.3 all-gather.5
